TPU v7x, 32 devices: a whole 2x2x4 slice. The times are simulated.
32 devices in a mesh: gx: 4 (over x, core), gy: 2 (over y), gz: 4 (over z).
Axes of the slice: x: 2, y: 2, z: 4, core: 2. Of those that a mesh axis runs over, the one named last changes fastest.
Arguments:
- displace: float32 [3, 8, 16, 512], P(None, 'gx', 'gy', 'gz'), may hold values from -0.15 to 0.15
- occupied: int32 [8, 16, 512], P('gx', 'gy', 'gz'), may hold values from 0 to 1, as said below
- strength: float32 [8, 16, 512], P('gx', 'gy', 'gz'), may hold values from 0.5 to 2
Outputs:
- force: float32 [3, 8, 16, 512], P(None, 'gx', 'gy', 'gz')
- energy: float32 [8, 16, 512], P('gx', 'gy', 'gz')
Inputs may be any that keep to these rules, and one draw needn't show every extreme that they name: `occupied`: 0 for a vacancy, 1 for an atom; the share of vacancies differs from domain to domain.
All inputs are finite; a program needn't handle non-finite values.
Results may differ from a plain program's by a relative error of at most 0.00017.
Values sent between devices are 32-bit elements; how exact they have to be, the bound alone decides.
A program may use at most 64 MiB of HBM per device.

v0:
```python
import jax
import jax.numpy as jnp
from jax import lax
from jax.sharding import PartitionSpec as P

ITERS = 3


RADIUS_SQ = 4.84
STEP = 0.02
FULL_OFFSETS = [
    (first, second, third)
    for first in (-1, 0, 1)
    for second in (-1, 0, 1)
    for third in (-1, 0, 1)
    if (first, second, third) != (0, 0, 0)
]


def padded_2(cells, sides, width):
    for axis, dim in sides:
        count = lax.axis_size(axis)
        ends = count - 1
        head = lax.slice_in_dim(cells, 0, width, axis=dim)
        tail = lax.slice_in_dim(cells, cells.shape[dim] - width, cells.shape[dim], axis=dim)
        cells = jnp.concatenate(
            [
                lax.ppermute(tail, axis, [(i, (i + 1) % count) for i in range(ends)]),
                cells,
                lax.ppermute(head, axis, [((i + 1) % count, i) for i in range(ends)]),
            ],
            axis=dim,
        )
    return cells


def cutoff(distance):
    inside = 1.0 - distance * distance / RADIUS_SQ
    return inside * inside


def cutoff_slope(distance):
    inside = 1.0 - distance * distance / RADIUS_SQ
    return -4.0 * inside * distance / RADIUS_SQ


def density(distance):
    return jnp.exp(-2.0 * (distance - 1.0)) * cutoff(distance)


def density_slope(distance):
    growth = jnp.exp(-2.0 * (distance - 1.0))
    return growth * (cutoff_slope(distance) - 2.0 * cutoff(distance))


def repulse(distance):
    return 0.5 * jnp.exp(-4.0 * (distance - 1.0)) * cutoff(distance)


def repulse_slope(distance):
    growth = 0.5 * jnp.exp(-4.0 * (distance - 1.0))
    return growth * (cutoff_slope(distance) - 4.0 * cutoff(distance))


def window_at(padded, base, offset, extent):
    return padded[
        ...,
        base + offset[0] : base + offset[0] + extent[0],
        base + offset[1] : base + offset[1] + extent[1],
        base + offset[2] : base + offset[2] + extent[2],
    ]


def pair_geometry(around_disp, center, base, offset, extent):
    lattice = jnp.array(offset, jnp.float32).reshape(3, 1, 1, 1)
    separation = lattice + window_at(around_disp, base, offset, extent) - center
    distance = jnp.sqrt(jnp.sum(separation * separation, axis=0))
    return (separation, distance)


def full_density(around_disp, around_weight, center, base, extent):
    total = jnp.zeros(tuple(extent), jnp.float32)
    for offset in FULL_OFFSETS:
        separation, distance = pair_geometry(around_disp, center, base, offset, extent)
        total = total + window_at(around_weight, base, offset, extent) * density(distance)
    return total


def full_forces(
    around_disp, around_weight, slopes, slope_base, center, base, extent, slope, weight
):
    force = jnp.zeros(center.shape, jnp.float32)
    pair_sum = jnp.zeros(tuple(extent), jnp.float32)
    for offset in FULL_OFFSETS:
        separation, distance = pair_geometry(around_disp, center, base, offset, extent)
        near_weight = window_at(around_weight, base, offset, extent)
        near_slope = window_at(slopes, slope_base, offset, extent)
        coupling = (slope * near_weight + near_slope * weight) * density_slope(
            distance
        ) + weight * near_weight * repulse_slope(distance)
        force = force + coupling / distance * separation
        pair_sum = pair_sum + near_weight * repulse(distance)
    return (force, 0.5 * weight * pair_sum)


def body(displace, occupied, strength):
    extent = occupied.shape
    occupancy = occupied.astype(jnp.float32)
    weight = occupancy * strength
    padded_shape = (extent[0] + 2, extent[1] + 2, extent[2] + 2)

    def evaluate(current):
        packed = jnp.concatenate([current, weight[None], occupancy[None]], axis=0)
        beside_all = padded_2(packed, (("gx", 1), ("gy", 2), ("gz", 3)), 2)
        around_disp = beside_all[:3]
        around_weight = beside_all[3]
        cycle_center = around_disp[:, 1 : extent[0] + 3, 1 : extent[1] + 3, 1 : extent[2] + 3]
        cycle_density = full_density(around_disp, around_weight, cycle_center, 1, padded_shape)
        cycle_occupancy = beside_all[4, 1 : extent[0] + 3, 1 : extent[1] + 3, 1 : extent[2] + 3]
        cycle_slope = cycle_occupancy * -0.5 * lax.rsqrt(1.0 + cycle_density)
        density_sum = cycle_density[1 : extent[0] + 1, 1 : extent[1] + 1, 1 : extent[2] + 1]
        slope = occupancy * -0.5 * lax.rsqrt(1.0 + density_sum)
        force, pair_energy = full_forces(
            around_disp, around_weight, cycle_slope, 1, current, 2, extent, slope, weight
        )
        energy = occupancy * -jnp.sqrt(1.0 + density_sum) + pair_energy
        return (force, energy)

    current = displace
    force, energy = evaluate(current)
    for step in range(ITERS - 1):
        current = current + STEP * force
        force, energy = evaluate(current)
    return (force, energy)


def solution(mesh):
    in_specs = (P(None, "gx", "gy", "gz"), P("gx", "gy", "gz"), P("gx", "gy", "gz"))
    out_specs = (P(None, "gx", "gy", "gz"), P("gx", "gy", "gz"))
    return jax.shard_map(body, mesh=mesh, in_specs=in_specs, out_specs=out_specs, check_vma=False)
```

profile of v0, /device:TPU:14, one launch (start us, length us, event | category | flops | bytes accessed | tf_op | source)
XLA Modules:
  0.0 97.4 jit_solution(14682878602944601669)
XLA Ops:
  1.4 1.9 %collective-permute-start.1 = (f32[5,2,8,128]{3,2,1,0:T(8,128)S(1)}, f32[5,2,8,128]{3,2,1,0:T(8,128)S(1)}, u32[]{:S(2)}, u32[]{:S(2)}) collective-permute-start(f32[5,2,8,128]{3,2,1,0:T(8,128)S(1)} %pad_maximum_fusion.44), channel_id=1, source_target_pairs={{8,0},{16,8},{24,16},{9,1},{17,9},{25,17},{10,2},{18,10},{26,18},{... | collective-permute-start | bytes 122888 | tf_op jit(solution)/shard_map/ppermute | solution.py:30
  3.4 2.4 %collective-permute-start = (f32[5,2,8,128]{3,2,1,0:T(8,128)S(1)}, f32[5,2,8,128]{3,2,1,0:T(8,128)S(1)}, u32[]{:S(2)}, u32[]{:S(2)}) collective-permute-start(f32[5,2,8,128]{3,2,1,0:T(8,128)S(1)} %pad_maximum_fusion.44), channel_id=1, source_target_pairs={{0,8},{8,16},{16,24},{1,9},{9,17},{17,25},{2,10},{10,18},{18,26},{... | collective-permute-start | bytes 122888 | tf_op jit(solution)/shard_map/ppermute | solution.py:28
  5.8 2.9 %collective-permute-done = f32[5,2,8,128]{3,2,1,0:T(8,128)S(1)} collective-permute-done((f32[5,2,8,128]{3,2,1,0:T(8,128)S(1)}, f32[5,2,8,128]{3,2,1,0:T(8,128)S(1)}, u32[]{:S(2)}, u32[]{:S(2)}) %collective-permute-start) | collective-permute-done | bytes 40992 | tf_op jit(solution)/shard_map/ppermute | solution.py:28
  8.8 2.4 %collective-permute-start.3 = (f32[5,6,2,128]{3,2,1,0:T(2,128)S(1)}, f32[5,6,2,128]{3,2,1,0:T(2,128)S(1)}, u32[]{:S(2)}, u32[]{:S(2)}) collective-permute-start(f32[5,6,2,128]{3,2,1,0:T(2,128)S(1)} %get-tuple-element.295), channel_id=1, source_target_pairs={{4,0},{5,1},{6,2},{7,3},{12,8},{13,9},{14,10},{15,11},{20,16},{21,... | collective-permute-start | bytes 92168 | tf_op jit(solution)/shard_map/ppermute | solution.py:30
  12.7 4.2 %collective-permute-done.2 = f32[5,6,2,128]{3,2,1,0:T(2,128)S(1)} collective-permute-done((f32[5,6,2,128]{3,2,1,0:T(2,128)S(1)}, f32[5,6,2,128]{3,2,1,0:T(2,128)S(1)}, u32[]{:S(2)}, u32[]{:S(2)}) %collective-permute-start.2) | collective-permute-done | bytes 30752 | tf_op jit(solution)/shard_map/ppermute | solution.py:28
  17.1 3.5 %collective-permute-start.4 = (f32[5,6,12,2]{3,2,1,0:T(8,128)S(1)}, f32[5,6,12,2]{3,2,1,0:T(8,128)S(1)}, u32[]{:S(2)}, u32[]{:S(2)}) collective-permute-start(f32[5,6,12,2]{3,2,1,0:T(8,128)S(1)} %get-tuple-element.201), channel_id=1, source_target_pairs={{0,1},{1,2},{2,3},{4,5},{5,6},{6,7},{8,9},{9,10},{10,11},{12,13},{... | collective-permute-start | bytes 8648 | tf_op jit(solution)/shard_map/ppermute | solution.py:28
  20.6 2.4 %collective-permute-start.5 = (f32[5,6,12,2]{3,2,1,0:T(8,128)S(1)}, f32[5,6,12,2]{3,2,1,0:T(8,128)S(1)}, u32[]{:S(2)}, u32[]{:S(2)}) collective-permute-start(f32[5,6,12,2]{3,2,1,0:T(8,128)S(1)} %get-tuple-element.202), channel_id=1, source_target_pairs={{1,0},{2,1},{3,2},{5,4},{6,5},{7,6},{9,8},{10,9},{11,10},{13,12},{... | collective-permute-start | bytes 8648 | tf_op jit(solution)/shard_map/ppermute | solution.py:30
  25.2 3.5 %collective-permute-done.5 = f32[5,6,12,2]{3,2,1,0:T(8,128)S(1)} collective-permute-done((f32[5,6,12,2]{3,2,1,0:T(8,128)S(1)}, f32[5,6,12,2]{3,2,1,0:T(8,128)S(1)}, u32[]{:S(2)}, u32[]{:S(2)}) %collective-permute-start.5) | collective-permute-done | bytes 2912 | tf_op jit(solution)/shard_map/ppermute | solution.py:30
  35.3 1.9 %collective-permute-start.7 = (f32[5,2,8,128]{3,2,1,0:T(8,128)S(1)}, f32[5,2,8,128]{3,2,1,0:T(8,128)S(1)}, u32[]{:S(2)}, u32[]{:S(2)}) collective-permute-start(f32[5,2,8,128]{3,2,1,0:T(8,128)S(1)} %pad_maximum_fusion.43), channel_id=1, source_target_pairs={{8,0},{16,8},{24,16},{9,1},{17,9},{25,17},{10,2},{18,10},{26,18},{... | collective-permute-start | bytes 122888 | tf_op jit(solution)/shard_map/ppermute | solution.py:30
  37.3 2.4 %collective-permute-start.6 = (f32[5,2,8,128]{3,2,1,0:T(8,128)S(1)}, f32[5,2,8,128]{3,2,1,0:T(8,128)S(1)}, u32[]{:S(2)}, u32[]{:S(2)}) collective-permute-start(f32[5,2,8,128]{3,2,1,0:T(8,128)S(1)} %pad_maximum_fusion.43), channel_id=1, source_target_pairs={{0,8},{8,16},{16,24},{1,9},{9,17},{17,25},{2,10},{10,18},{18,26},{... | collective-permute-start | bytes 122888 | tf_op jit(solution)/shard_map/ppermute | solution.py:28
  39.7 2.9 %collective-permute-done.6 = f32[5,2,8,128]{3,2,1,0:T(8,128)S(1)} collective-permute-done((f32[5,2,8,128]{3,2,1,0:T(8,128)S(1)}, f32[5,2,8,128]{3,2,1,0:T(8,128)S(1)}, u32[]{:S(2)}, u32[]{:S(2)}) %collective-permute-start.6) | collective-permute-done | bytes 40992 | tf_op jit(solution)/shard_map/ppermute | solution.py:28
  45.8 4.2 %collective-permute-done.8 = f32[5,6,2,128]{3,2,1,0:T(2,128)S(1)} collective-permute-done((f32[5,6,2,128]{3,2,1,0:T(2,128)S(1)}, f32[5,6,2,128]{3,2,1,0:T(2,128)S(1)}, u32[]{:S(2)}, u32[]{:S(2)}) %collective-permute-start.8) | collective-permute-done | bytes 30752 | tf_op jit(solution)/shard_map/ppermute | solution.py:28
  50.2 3.5 %collective-permute-start.10 = (f32[5,6,12,2]{3,2,1,0:T(8,128)S(1)}, f32[5,6,12,2]{3,2,1,0:T(8,128)S(1)}, u32[]{:S(2)}, u32[]{:S(2)}) collective-permute-start(f32[5,6,12,2]{3,2,1,0:T(8,128)S(1)} %get-tuple-element.199), channel_id=1, source_target_pairs={{0,1},{1,2},{2,3},{4,5},{5,6},{6,7},{8,9},{9,10},{10,11},{12,13},{... | collective-permute-start | bytes 8648 | tf_op jit(solution)/shard_map/ppermute | solution.py:28
  53.7 2.4 %collective-permute-start.11 = (f32[5,6,12,2]{3,2,1,0:T(8,128)S(1)}, f32[5,6,12,2]{3,2,1,0:T(8,128)S(1)}, u32[]{:S(2)}, u32[]{:S(2)}) collective-permute-start(f32[5,6,12,2]{3,2,1,0:T(8,128)S(1)} %get-tuple-element.200), channel_id=1, source_target_pairs={{1,0},{2,1},{3,2},{5,4},{6,5},{7,6},{9,8},{10,9},{11,10},{13,12},{... | collective-permute-start | bytes 8648 | tf_op jit(solution)/shard_map/ppermute | solution.py:30
  56.2 2.1 %collective-permute-done.10 = f32[5,6,12,2]{3,2,1,0:T(8,128)S(1)} collective-permute-done((f32[5,6,12,2]{3,2,1,0:T(8,128)S(1)}, f32[5,6,12,2]{3,2,1,0:T(8,128)S(1)}, u32[]{:S(2)}, u32[]{:S(2)}) %collective-permute-start.10) | collective-permute-done | bytes 2912 | tf_op jit(solution)/shard_map/ppermute | solution.py:28
  58.3 3.5 %collective-permute-done.11 = f32[5,6,12,2]{3,2,1,0:T(8,128)S(1)} collective-permute-done((f32[5,6,12,2]{3,2,1,0:T(8,128)S(1)}, f32[5,6,12,2]{3,2,1,0:T(8,128)S(1)}, u32[]{:S(2)}, u32[]{:S(2)}) %collective-permute-start.11) | collective-permute-done | bytes 2912 | tf_op jit(solution)/shard_map/ppermute | solution.py:30
  66.3 1.9 %collective-permute-start.13 = (f32[5,2,8,128]{3,2,1,0:T(8,128)S(1)}, f32[5,2,8,128]{3,2,1,0:T(8,128)S(1)}, u32[]{:S(2)}, u32[]{:S(2)}) collective-permute-start(f32[5,2,8,128]{3,2,1,0:T(8,128)S(1)} %pad_maximum_fusion.42), channel_id=1, source_target_pairs={{8,0},{16,8},{24,16},{9,1},{17,9},{25,17},{10,2},{18,10},{26,18},{... | collective-permute-start | bytes 122888 | tf_op jit(solution)/shard_map/ppermute | solution.py:30
  68.2 2.4 %collective-permute-start.12 = (f32[5,2,8,128]{3,2,1,0:T(8,128)S(1)}, f32[5,2,8,128]{3,2,1,0:T(8,128)S(1)}, u32[]{:S(2)}, u32[]{:S(2)}) collective-permute-start(f32[5,2,8,128]{3,2,1,0:T(8,128)S(1)} %pad_maximum_fusion.42), channel_id=1, source_target_pairs={{0,8},{8,16},{16,24},{1,9},{9,17},{17,25},{2,10},{10,18},{18,26},{... | collective-permute-start | bytes 122888 | tf_op jit(solution)/shard_map/ppermute | solution.py:28
  70.6 2.9 %collective-permute-done.12 = f32[5,2,8,128]{3,2,1,0:T(8,128)S(1)} collective-permute-done((f32[5,2,8,128]{3,2,1,0:T(8,128)S(1)}, f32[5,2,8,128]{3,2,1,0:T(8,128)S(1)}, u32[]{:S(2)}, u32[]{:S(2)}) %collective-permute-start.12) | collective-permute-done | bytes 40992 | tf_op jit(solution)/shard_map/ppermute | solution.py:28
  76.7 4.2 %collective-permute-done.14 = f32[5,6,2,128]{3,2,1,0:T(2,128)S(1)} collective-permute-done((f32[5,6,2,128]{3,2,1,0:T(2,128)S(1)}, f32[5,6,2,128]{3,2,1,0:T(2,128)S(1)}, u32[]{:S(2)}, u32[]{:S(2)}) %collective-permute-start.14) | collective-permute-done | bytes 30752 | tf_op jit(solution)/shard_map/ppermute | solution.py:28
  81.2 2.4 %collective-permute-start.17 = (f32[5,6,12,2]{3,2,1,0:T(8,128)S(1)}, f32[5,6,12,2]{3,2,1,0:T(8,128)S(1)}, u32[]{:S(2)}, u32[]{:S(2)}) collective-permute-start(f32[5,6,12,2]{3,2,1,0:T(8,128)S(1)} %get-tuple-element.198), channel_id=1, source_target_pairs={{1,0},{2,1},{3,2},{5,4},{6,5},{7,6},{9,8},{10,9},{11,10},{13,12},{... | collective-permute-start | bytes 8648 | tf_op jit(solution)/shard_map/ppermute | solution.py:30
  83.5 3.7 %collective-permute-start.16 = (f32[5,6,12,2]{3,2,1,0:T(8,128)S(1)}, f32[5,6,12,2]{3,2,1,0:T(8,128)S(1)}, u32[]{:S(2)}, u32[]{:S(2)}) collective-permute-start(f32[5,6,12,2]{3,2,1,0:T(8,128)S(1)} %get-tuple-element.197), channel_id=1, source_target_pairs={{0,1},{1,2},{2,3},{4,5},{5,6},{6,7},{8,9},{9,10},{10,11},{12,13},{... | collective-permute-start | bytes 8648 | tf_op jit(solution)/shard_map/ppermute | solution.py:28
  87.3 1.9 %collective-permute-done.17 = f32[5,6,12,2]{3,2,1,0:T(8,128)S(1)} collective-permute-done((f32[5,6,12,2]{3,2,1,0:T(8,128)S(1)}, f32[5,6,12,2]{3,2,1,0:T(8,128)S(1)}, u32[]{:S(2)}, u32[]{:S(2)}) %collective-permute-start.17) | collective-permute-done | bytes 2912 | tf_op jit(solution)/shard_map/ppermute | solution.py:30
  89.2 2.4 %collective-permute-done.16 = f32[5,6,12,2]{3,2,1,0:T(8,128)S(1)} collective-permute-done((f32[5,6,12,2]{3,2,1,0:T(8,128)S(1)}, f32[5,6,12,2]{3,2,1,0:T(8,128)S(1)}, u32[]{:S(2)}, u32[]{:S(2)}) %collective-permute-start.16) | collective-permute-done | bytes 2912 | tf_op jit(solution)/shard_map/ppermute | solution.py:28
  (144 shorter events, 28.2 us)
Async XLA Ops:
  0.6 0.8 copy-start.1
  0.6 0.8 copy-start.26
  0.6 0.8 copy-start
  1.4 4.3 %collective-permute-start.1 = (f32[5,2,8,128]{3,2,1,0:T(8,128)S(1)}, f32[5,2,8,128]{3,2,1,0:T(8,128)S(1)}, u32[]{:S(2)}, u32[]{:S(2)}) collective-permute-start(f32[5,2,8,128]{3,2,1,0:T(8,128)S(1)} %pad_maximum_fusion.44), channel_id=1, source_target_pairs={{8,0},{16,8},{24,16},{9,1},{17,9},{25,17},{10,2},{18,10},{26,18},{... | collective-permute-start | bytes 122888 | tf_op jit(solution)/shard_map/ppermute | solution.py:30
  3.4 5.3 %collective-permute-start = (f32[5,2,8,128]{3,2,1,0:T(8,128)S(1)}, f32[5,2,8,128]{3,2,1,0:T(8,128)S(1)}, u32[]{:S(2)}, u32[]{:S(2)}) collective-permute-start(f32[5,2,8,128]{3,2,1,0:T(8,128)S(1)} %pad_maximum_fusion.44), channel_id=1, source_target_pairs={{0,8},{8,16},{16,24},{1,9},{9,17},{17,25},{2,10},{10,18},{18,26},{... | collective-permute-start | bytes 122888 | tf_op jit(solution)/shard_map/ppermute | solution.py:28
  8.7 3.7 %copy-start.7 = (f32[3]{0:T(128)S(1)}, f32[3]{0:T(128)}, u32[]{:S(2)}) copy-start(f32[3]{0:T(128)} %constant.471.clone) | copy-start | bytes 40
  8.7 3.7 %copy-start.8 = (f32[3]{0:T(128)S(1)}, f32[3]{0:T(128)}, u32[]{:S(2)}) copy-start(f32[3]{0:T(128)} %constant.488.clone) | copy-start | bytes 40
  8.8 4.0 %collective-permute-start.3 = (f32[5,6,2,128]{3,2,1,0:T(2,128)S(1)}, f32[5,6,2,128]{3,2,1,0:T(2,128)S(1)}, u32[]{:S(2)}, u32[]{:S(2)}) collective-permute-start(f32[5,6,2,128]{3,2,1,0:T(2,128)S(1)} %get-tuple-element.295), channel_id=1, source_target_pairs={{4,0},{5,1},{6,2},{7,3},{12,8},{13,9},{14,10},{15,11},{20,16},{21,... | collective-permute-start | bytes 92168 | tf_op jit(solution)/shard_map/ppermute | solution.py:30
  11.2 5.8 %collective-permute-start.2 = (f32[5,6,2,128]{3,2,1,0:T(2,128)S(1)}, f32[5,6,2,128]{3,2,1,0:T(2,128)S(1)}, u32[]{:S(2)}, u32[]{:S(2)}) collective-permute-start(f32[5,6,2,128]{3,2,1,0:T(2,128)S(1)} %get-tuple-element.294), channel_id=1, source_target_pairs={{0,4},{1,5},{2,6},{3,7},{8,12},{9,13},{10,14},{11,15},{16,20},{17,... | collective-permute-start | bytes 92168 | tf_op jit(solution)/shard_map/ppermute | solution.py:28
  17.1 8.1 %collective-permute-start.4 = (f32[5,6,12,2]{3,2,1,0:T(8,128)S(1)}, f32[5,6,12,2]{3,2,1,0:T(8,128)S(1)}, u32[]{:S(2)}, u32[]{:S(2)}) collective-permute-start(f32[5,6,12,2]{3,2,1,0:T(8,128)S(1)} %get-tuple-element.201), channel_id=1, source_target_pairs={{0,1},{1,2},{2,3},{4,5},{5,6},{6,7},{8,9},{9,10},{10,11},{12,13},{... | collective-permute-start | bytes 8648 | tf_op jit(solution)/shard_map/ppermute | solution.py:28
  20.6 8.1 %collective-permute-start.5 = (f32[5,6,12,2]{3,2,1,0:T(8,128)S(1)}, f32[5,6,12,2]{3,2,1,0:T(8,128)S(1)}, u32[]{:S(2)}, u32[]{:S(2)}) collective-permute-start(f32[5,6,12,2]{3,2,1,0:T(8,128)S(1)} %get-tuple-element.202), channel_id=1, source_target_pairs={{1,0},{2,1},{3,2},{5,4},{6,5},{7,6},{9,8},{10,9},{11,10},{13,12},{... | collective-permute-start | bytes 8648 | tf_op jit(solution)/shard_map/ppermute | solution.py:30
  32.1 0.7 copy-start.25
  35.3 4.3 %collective-permute-start.7 = (f32[5,2,8,128]{3,2,1,0:T(8,128)S(1)}, f32[5,2,8,128]{3,2,1,0:T(8,128)S(1)}, u32[]{:S(2)}, u32[]{:S(2)}) collective-permute-start(f32[5,2,8,128]{3,2,1,0:T(8,128)S(1)} %pad_maximum_fusion.43), channel_id=1, source_target_pairs={{8,0},{16,8},{24,16},{9,1},{17,9},{25,17},{10,2},{18,10},{26,18},{... | collective-permute-start | bytes 122888 | tf_op jit(solution)/shard_map/ppermute | solution.py:30
  37.3 5.3 %collective-permute-start.6 = (f32[5,2,8,128]{3,2,1,0:T(8,128)S(1)}, f32[5,2,8,128]{3,2,1,0:T(8,128)S(1)}, u32[]{:S(2)}, u32[]{:S(2)}) collective-permute-start(f32[5,2,8,128]{3,2,1,0:T(8,128)S(1)} %pad_maximum_fusion.43), channel_id=1, source_target_pairs={{0,8},{8,16},{16,24},{1,9},{9,17},{17,25},{2,10},{10,18},{18,26},{... | collective-permute-start | bytes 122888 | tf_op jit(solution)/shard_map/ppermute | solution.py:28
  42.6 3.2 %collective-permute-start.9 = (f32[5,6,2,128]{3,2,1,0:T(2,128)S(1)}, f32[5,6,2,128]{3,2,1,0:T(2,128)S(1)}, u32[]{:S(2)}, u32[]{:S(2)}) collective-permute-start(f32[5,6,2,128]{3,2,1,0:T(2,128)S(1)} %get-tuple-element.291), channel_id=1, source_target_pairs={{4,0},{5,1},{6,2},{7,3},{12,8},{13,9},{14,10},{15,11},{20,16},{21,... | collective-permute-start | bytes 92168 | tf_op jit(solution)/shard_map/ppermute | solution.py:30
  44.2 5.8 %collective-permute-start.8 = (f32[5,6,2,128]{3,2,1,0:T(2,128)S(1)}, f32[5,6,2,128]{3,2,1,0:T(2,128)S(1)}, u32[]{:S(2)}, u32[]{:S(2)}) collective-permute-start(f32[5,6,2,128]{3,2,1,0:T(2,128)S(1)} %get-tuple-element.290), channel_id=1, source_target_pairs={{0,4},{1,5},{2,6},{3,7},{8,12},{9,13},{10,14},{11,15},{16,20},{17,... | collective-permute-start | bytes 92168 | tf_op jit(solution)/shard_map/ppermute | solution.py:28
  50.2 8.1 %collective-permute-start.10 = (f32[5,6,12,2]{3,2,1,0:T(8,128)S(1)}, f32[5,6,12,2]{3,2,1,0:T(8,128)S(1)}, u32[]{:S(2)}, u32[]{:S(2)}) collective-permute-start(f32[5,6,12,2]{3,2,1,0:T(8,128)S(1)} %get-tuple-element.199), channel_id=1, source_target_pairs={{0,1},{1,2},{2,3},{4,5},{5,6},{6,7},{8,9},{9,10},{10,11},{12,13},{... | collective-permute-start | bytes 8648 | tf_op jit(solution)/shard_map/ppermute | solution.py:28
  53.7 8.1 %collective-permute-start.11 = (f32[5,6,12,2]{3,2,1,0:T(8,128)S(1)}, f32[5,6,12,2]{3,2,1,0:T(8,128)S(1)}, u32[]{:S(2)}, u32[]{:S(2)}) collective-permute-start(f32[5,6,12,2]{3,2,1,0:T(8,128)S(1)} %get-tuple-element.200), channel_id=1, source_target_pairs={{1,0},{2,1},{3,2},{5,4},{6,5},{7,6},{9,8},{10,9},{11,10},{13,12},{... | collective-permute-start | bytes 8648 | tf_op jit(solution)/shard_map/ppermute | solution.py:30
  66.3 4.3 %collective-permute-start.13 = (f32[5,2,8,128]{3,2,1,0:T(8,128)S(1)}, f32[5,2,8,128]{3,2,1,0:T(8,128)S(1)}, u32[]{:S(2)}, u32[]{:S(2)}) collective-permute-start(f32[5,2,8,128]{3,2,1,0:T(8,128)S(1)} %pad_maximum_fusion.42), channel_id=1, source_target_pairs={{8,0},{16,8},{24,16},{9,1},{17,9},{25,17},{10,2},{18,10},{26,18},{... | collective-permute-start | bytes 122888 | tf_op jit(solution)/shard_map/ppermute | solution.py:30
  68.2 5.3 %collective-permute-start.12 = (f32[5,2,8,128]{3,2,1,0:T(8,128)S(1)}, f32[5,2,8,128]{3,2,1,0:T(8,128)S(1)}, u32[]{:S(2)}, u32[]{:S(2)}) collective-permute-start(f32[5,2,8,128]{3,2,1,0:T(8,128)S(1)} %pad_maximum_fusion.42), channel_id=1, source_target_pairs={{0,8},{8,16},{16,24},{1,9},{9,17},{17,25},{2,10},{10,18},{18,26},{... | collective-permute-start | bytes 122888 | tf_op jit(solution)/shard_map/ppermute | solution.py:28
  73.6 3.2 %collective-permute-start.15 = (f32[5,6,2,128]{3,2,1,0:T(2,128)S(1)}, f32[5,6,2,128]{3,2,1,0:T(2,128)S(1)}, u32[]{:S(2)}, u32[]{:S(2)}) collective-permute-start(f32[5,6,2,128]{3,2,1,0:T(2,128)S(1)} %get-tuple-element.287), channel_id=1, source_target_pairs={{4,0},{5,1},{6,2},{7,3},{12,8},{13,9},{14,10},{15,11},{20,16},{21,... | collective-permute-start | bytes 92168 | tf_op jit(solution)/shard_map/ppermute | solution.py:30
  75.2 5.8 %collective-permute-start.14 = (f32[5,6,2,128]{3,2,1,0:T(2,128)S(1)}, f32[5,6,2,128]{3,2,1,0:T(2,128)S(1)}, u32[]{:S(2)}, u32[]{:S(2)}) collective-permute-start(f32[5,6,2,128]{3,2,1,0:T(2,128)S(1)} %get-tuple-element.286), channel_id=1, source_target_pairs={{0,4},{1,5},{2,6},{3,7},{8,12},{9,13},{10,14},{11,15},{16,20},{17,... | collective-permute-start | bytes 92168 | tf_op jit(solution)/shard_map/ppermute | solution.py:28
  81.2 8.1 %collective-permute-start.17 = (f32[5,6,12,2]{3,2,1,0:T(8,128)S(1)}, f32[5,6,12,2]{3,2,1,0:T(8,128)S(1)}, u32[]{:S(2)}, u32[]{:S(2)}) collective-permute-start(f32[5,6,12,2]{3,2,1,0:T(8,128)S(1)} %get-tuple-element.198), channel_id=1, source_target_pairs={{1,0},{2,1},{3,2},{5,4},{6,5},{7,6},{9,8},{10,9},{11,10},{13,12},{... | collective-permute-start | bytes 8648 | tf_op jit(solution)/shard_map/ppermute | solution.py:30
  83.5 8.1 %collective-permute-start.16 = (f32[5,6,12,2]{3,2,1,0:T(8,128)S(1)}, f32[5,6,12,2]{3,2,1,0:T(8,128)S(1)}, u32[]{:S(2)}, u32[]{:S(2)}) collective-permute-start(f32[5,6,12,2]{3,2,1,0:T(8,128)S(1)} %get-tuple-element.197), channel_id=1, source_target_pairs={{0,1},{1,2},{2,3},{4,5},{5,6},{6,7},{8,9},{9,10},{10,11},{12,13},{... | collective-permute-start | bytes 8648 | tf_op jit(solution)/shard_map/ppermute | solution.py:28
  (21 other events, 14.1 us)
where the time goes:
time: 98 us; the launch traced here: 97.4 us
  starting transfers between devices  40.2 us (41%)
  waiting for transfers between devices  36.6 us (37%)
  other arithmetic  16 us (16%)
  local copies, waits for them, and re-layouts  3.24 us (3%)
  between operations  1.42 us (1%)
    ppermute x9, waiting for transfers between devices, padded_2(): lax.ppermute(tail, axis, [(i, (i + 1) % count) for i in range(ends)])  27.2 us
    ppermute x9, starting transfers between devices, padded_2(): lax.ppermute(tail, axis, [(i, (i + 1) % count) for i in range(ends)])  21.7 us
    ppermute x9, starting transfers between devices, padded_2(): lax.ppermute(head, axis, [((i + 1) % count, i) for i in range(ends)])  18.5 us
    ppermute x9, waiting for transfers between devices, padded_2(): lax.ppermute(head, axis, [((i + 1) % count, i) for i in range(ends)])  9.41 us
    reduce_sum x24, other arithmetic, pair_geometry(): distance = jnp.sqrt(jnp.sum(separation * separation, axis=0))  5.42 us
    mul x3, other arithmetic, evaluate(): cycle_slope = cycle_occupancy * -0.5 * lax.rsqrt(1.0 + cycle_density)  3.31 us
    unnamed x54, local copies, waits for them, and re-layouts  2.78 us
    concatenate x15, other arithmetic, padded_2(): jnp.concatenate([lax.ppermute(tail, axis, [(i, (i + 1) % count) for i in...  2.47 us
  transfers between devices with their start and end apart: 18, of which 15 were waited for; matrix products, arithmetic and copies ran while one was open for 1% of the time, Pallas kernels for 0%

commit v1 on v0

v1 whole, which is shorter than its diff:
```python
import functools

import jax
import jax.numpy as jnp
from jax import lax
from jax.experimental import pallas as pl
from jax.experimental.pallas import tpu as pltpu
from jax.sharding import PartitionSpec as P

ITERS = 3
RADIUS_SQ = 4.84
STEP = 0.02
AXES = ("gx", "gy", "gz")
MESH = pl.DeviceIdType.MESH
LANES = 128
PLANE = [(dx, dy) for dx in (-1, 0, 1) for dy in (-1, 0, 1)]
NEAR = sorted(
    ((dx, dy, dz) for dx, dy in PLANE for dz in (-1, 0, 1) if (dx, dy, dz) != (0, 0, 0)),
    key=lambda o: (-sum(abs(a) for a in o), o),
)
SLOT = {o: i for i, o in enumerate(NEAR)}


def minus(o):
    return tuple(-a for a in o)


def up(rows):
    return -(-rows // 8) * 8


def kernel(sizes, counts, disp_ref, occ_ref, str_ref, force_ref, energy_ref,
           xs, ys, zs, xl, yl, zl, stage, near, cols, slopes, send_sem, recv_sem):
    cx, cy, cz = sizes
    pitch = cy + 4
    group = LANES // 4
    xu, yu = 3 * cx * cy, 3 * cx * 2
    xpanel, ypanel = xu, yu
    xw, yw = up(xu + 2), up(yu + 2)
    x_rows = (xs.shape[1], xw)
    y_rows = (ys.shape[2], yw)

    me = [lax.axis_index(axis) for axis in AXES]
    there = [[None if s == 0 else (m + s >= 0) & (m + s < n) for s in (-1, 0, 1)]
             for m, n in zip(me, counts)]

    def exists(o):
        tests = [there[a][o[a] + 1] for a in range(3) if o[a] != 0]
        return functools.reduce(lambda p, q: p & q, tests)

    def target(o):
        return {AXES[a]: me[a] + o[a] for a in range(3)}

    barrier = pltpu.get_barrier_semaphore()
    for o in NEAR:
        @pl.when(exists(o))
        def _(o=o):
            pl.semaphore_signal(barrier, inc=1, device_id=target(o), device_id_type=MESH)
    spans = [1 + (m > 0).astype(jnp.int32) + (m < n - 1).astype(jnp.int32)
             for m, n in zip(me, counts)]

    def ends(t, o):
        back = minus(o)
        if o[2] != 0:
            side = 0 if o[2] == 1 else 1
            src = zs.at[t, side]
            dst = zl.at[t, PLANE.index(back[:2]), side]
        elif o[1] != 0:
            rows = y_rows[0] if t == 0 else y_rows[1]
            side = 0 if o[1] == 1 else 1
            src = ys.at[t, side, pl.ds(0, rows)]
            dst = yl.at[t, back[0] + 1, side, pl.ds(0, rows)]
        else:
            rows = x_rows[0] if t == 0 else x_rows[1]
            src = xs.at[t, pl.ds(0, rows)]
            dst = xl.at[t, 0 if o[0] == 1 else 1, pl.ds(0, rows)]
        return pltpu.make_async_remote_copy(
            src_ref=src, dst_ref=dst, send_sem=send_sem.at[t, SLOT[o]],
            recv_sem=recv_sem.at[t, SLOT[back]], device_id=target(o), device_id_type=MESH)

    for o in NEAR:
        @pl.when(jnp.logical_not(exists(o)))
        def _(o=o):
            if o[2] != 0:
                spot = zl.at[:, PLANE.index(o[:2]), 0 if o[2] == -1 else 1]
            elif o[1] != 0:
                spot = yl.at[:, o[0] + 1, 0 if o[1] == -1 else 1]
            else:
                spot = xl.at[:, 0 if o[0] == -1 else 1]
            spot[...] = jnp.zeros(spot.shape, jnp.float32)

    stage[...] = jnp.zeros(stage.shape, jnp.float32)
    near[...] = jnp.zeros(near.shape, jnp.float32)
    cols[...] = jnp.zeros(cols.shape, jnp.float32)

    mine = [[disp_ref[q, x] for x in range(cx)] for q in range(3)]
    mine.append([occ_ref[x].astype(jnp.float32) * str_ref[x] for x in range(cx)])

    lane = lax.broadcasted_iota(jnp.int32, (8, LANES), 1)
    sub = lax.broadcasted_iota(jnp.int32, (8, LANES), 0)
    in_group = lax.rem(lax.rem(lane, group), pitch)
    depth = (lax.rem(sub, 4) - 1).astype(jnp.float32)
    middle = lax.rem(sub, 4) == 1
    hollow = lax.rem(sub, 4) == 3

    def moved(value, amount, axis=1):
        amount %= value.shape[axis]
        return value if amount == 0 else pltpu.roll(value, amount, axis)

    for t in range(ITERS):
        last = t == ITERS - 1
        for q in range(4):
            for x in range(cx):
                if q < 3 or t == 0:
                    stage[q * group + x * pitch + 2:q * group + x * pitch + 2 + cy] = mine[q][x]
        flipped = jnp.transpose(stage[...])
        head, tail = flipped[0:2], flipped[cz - 2:cz]
        first, final = flipped[0:1], flipped[cz - 1:cz]
        zs[t, 0] = tail
        zs[t, 1] = head
        for side in range(2):
            for q in range(4):
                if q == 3 and t > 0:
                    continue
                for x in range(cx):
                    base = (q * cx + x) * 2 if q < 3 else yw + x * 2
                    piece = mine[q][x]
                    ys[t, side, base:base + 2] = piece[cy - 2:cy] if side == 0 else piece[0:2]
            ys[t, side, ypanel:ypanel + 1] = first
            ys[t, side, ypanel + 1:ypanel + 2] = final
        for q in range(4):
            if q == 3 and t > 0:
                continue
            for x in range(cx):
                base = (q * cx + x) * cy if q < 3 else xw + x * cy
                xs[t, base:base + cy] = mine[q][x]
        xs[t, xpanel:xpanel + 1] = first
        xs[t, xpanel + 1:xpanel + 2] = final

        if t == 0:
            pl.semaphore_wait(barrier, spans[0] * spans[1] * spans[2] - 1)
        for o in NEAR:
            @pl.when(exists(o))
            def _(o=o):
                ends(t, o).start()
        for o in reversed(NEAR):
            @pl.when(exists(o))
            def _(o=o):
                ends(t, minus(o)).wait_recv()

        quantities = range(4) if t == 0 else range(3)
        for q in quantities:
            for dx in (-1, 0, 1):
                for x in range(cx):
                    row = (cx * (dx + 1) + x) * pitch
                    if dx == 0:
                        piece = mine[q][x]
                    else:
                        base = (q * cx + x) * cy if q < 3 else xw + x * cy
                        piece = xl[t, 0 if dx == -1 else 1, base:base + cy]
                    near[1, q, row + 2:row + 2 + cy] = piece
                    base = (q * cx + x) * 2 if q < 3 else yw + x * 2
                    near[1, q, row:row + 2] = yl[t, dx + 1, 0, base:base + 2]
                    near[1, q, row + 2 + cy:row + 4 + cy] = yl[t, dx + 1, 1, base:base + 2]
        for j, (dx, dy) in enumerate(PLANE):
            cols[j, 0:2] = zl[t, j, 0]
            cols[j, 5:7] = zl[t, j, 1]
            if dy != 0:
                a = yl[t, dx + 1, 0 if dy == -1 else 1, ypanel:ypanel + 1]
                b = yl[t, dx + 1, 0 if dy == -1 else 1, ypanel + 1:ypanel + 2]
            elif dx != 0:
                a = xl[t, 0 if dx == -1 else 1, xpanel:xpanel + 1]
                b = xl[t, 0 if dx == -1 else 1, xpanel + 1:xpanel + 2]
            else:
                a, b = first, final
            cols[j, 2:3] = a
            cols[j, 4:5] = b
        joined = []
        for dx in (-1, 0, 1):
            low, mid, high = (cols[PLANE.index((dx, dy))] for dy in (-1, 0, 1))
            joined.append(jnp.where(in_group < 2, moved(low, -cy),
                                    jnp.where(in_group < 2 + cy, mid, moved(high, cy))))
        wide = cx * pitch
        edge = []
        for q in range(4):
            value = jnp.zeros((8, LANES), jnp.float32)
            for i in (2, 1, 0):
                value = jnp.where(lane < wide * (i + 1),
                                  moved(joined[i], wide * i - group * q),
                                  value if i < 2 else 0.0)
            edge.append(value)

        turned = jnp.transpose(jnp.concatenate(edge, axis=0))
        rows = near.shape[2]
        wide_lane = lax.broadcasted_iota(jnp.int32, (rows, LANES), 1)
        for q in quantities:
            here = near[1, q]
            before = turned[0:rows, 8 * q + 1:8 * q + 2]
            after = turned[0:rows, 8 * q + 5:8 * q + 6]
            near[0, q] = jnp.where(wide_lane == 0, before, moved(here, 1))
            near[2, q] = jnp.where(wide_lane == cz - 1, after, moved(here, -1))

        center = [jnp.where(sub < 4, e[1:2], e[5:6]) for e in edge[:3]]
        total = jnp.zeros((8, LANES), jnp.float32)
        for dx, dy in PLANE:
            shift = -(dx * pitch + dy)
            far = [moved(e, shift) for e in edge]
            sx = far[0] - (center[0] - dx)
            sy = far[1] - (center[1] - dy)
            sz = far[2] - (center[2] - depth)
            square = sx * sx + sy * sy + sz * sz
            far_weight = far[3]
            if (dx, dy) == (0, 0):
                square = jnp.where(middle | hollow, 1.0, square)
                far_weight = jnp.where(middle | hollow, 0.0, far_weight)
            distance = square * lax.rsqrt(square)
            inside = 1.0 - square * (1.0 / RADIUS_SQ)
            total = total + far_weight * (jnp.exp(2.0 - 2.0 * distance) * (inside * inside))
        total = total + moved(total, 1, 0) + moved(total, -1, 0)
        edge_slope = jnp.where((edge[3] > 0.0) & middle, -0.5 * lax.rsqrt(1.0 + total), 0.0)
        turned_slope = jnp.transpose(edge_slope)

        begin = pitch + 1
        chunk = 16
        extent = up((cx + 2) * pitch + cy + 3 - begin)
        for start in range(begin, begin + extent, chunk):
            size = min(chunk, begin + extent - start)
            base = [[near[1, q, start:start + size] - s for s in (-1.0, 0.0, 1.0)] for q in range(3)]
            total = jnp.zeros((size, LANES), jnp.float32)
            for dx, dy in PLANE:
                row = start + dx * pitch + dy
                for dz in (-1, 0, 1):
                    if (dx, dy, dz) == (0, 0, 0):
                        continue
                    sx = near[dz + 1, 0, row:row + size] - base[0][dx + 1]
                    sy = near[dz + 1, 1, row:row + size] - base[1][dy + 1]
                    sz = near[dz + 1, 2, row:row + size] - base[2][dz + 1]
                    square = sx * sx + sy * sy + sz * sz
                    distance = square * lax.rsqrt(square)
                    inside = 1.0 - square * (1.0 / RADIUS_SQ)
                    total = total + near[dz + 1, 3, row:row + size] * (
                        jnp.exp(2.0 - 2.0 * distance) * (inside * inside))
            root = lax.rsqrt(1.0 + total)
            slope = jnp.where(near[1, 3, start:start + size] > 0.0, -0.5 * root, 0.0)
            slopes[1, start:start + size] = slope
            tall = lax.broadcasted_iota(jnp.int32, (size, LANES), 1)
            slopes[0, start:start + size] = jnp.where(
                tall == 0, turned_slope[start:start + size, 1:2], moved(slope, 1))
            slopes[2, start:start + size] = jnp.where(
                tall == cz - 1, turned_slope[start:start + size, 5:6], moved(slope, -1))
            if last:
                slopes[3, start:start + size] = (1.0 + total) * root

        for x in range(cx):
            start = (cx + x) * pitch + 2
            here = [mine[q][x] for q in range(3)]
            base = [[h - s for s in (-1.0, 0.0, 1.0)] for h in here]
            weight = mine[3][x]
            slope = slopes[1, start:start + cy]
            force = [jnp.zeros((cy, LANES), jnp.float32) for _ in range(3)]
            pair = jnp.zeros((cy, LANES), jnp.float32)
            for dx, dy in PLANE:
                row = start + dx * pitch + dy
                for dz in (-1, 0, 1):
                    if (dx, dy, dz) == (0, 0, 0):
                        continue
                    sx = near[dz + 1, 0, row:row + cy] - base[0][dx + 1]
                    sy = near[dz + 1, 1, row:row + cy] - base[1][dy + 1]
                    sz = near[dz + 1, 2, row:row + cy] - base[2][dz + 1]
                    far_weight = near[dz + 1, 3, row:row + cy]
                    far_slope = slopes[dz + 1, row:row + cy]
                    square = sx * sx + sy * sy + sz * sz
                    inverse = lax.rsqrt(square)
                    distance = square * inverse
                    inside = 1.0 - square * (1.0 / RADIUS_SQ)
                    cut = inside * inside
                    cut_slope = inside * distance * (-4.0 / RADIUS_SQ)
                    growth = jnp.exp(2.0 - 2.0 * distance)
                    steep = 0.5 * growth * growth
                    coupling = (slope * far_weight + far_slope * weight) * (
                        growth * (cut_slope - 2.0 * cut)) + weight * far_weight * (
                        steep * (cut_slope - 4.0 * cut))
                    scale = coupling * inverse
                    force = [force[0] + scale * sx, force[1] + scale * sy, force[2] + scale * sz]
                    if last:
                        pair = pair + far_weight * (steep * cut)
            if last:
                for q in range(3):
                    force_ref[q, x] = force[q]
                energy_ref[x] = 0.5 * weight * pair - jnp.where(
                    weight > 0.0, slopes[3, start:start + cy], 0.0)
            else:
                for q in range(3):
                    mine[q][x] = here[q] + STEP * force[q]

    for t in range(ITERS):
        for o in NEAR:
            @pl.when(exists(o))
            def _(o=o, t=t):
                ends(t, o).wait_send()


def solution(mesh):
    counts = tuple(mesh.shape[axis] for axis in AXES)

    def body(displace, occupied, strength):
        sizes = occupied.shape
        cx, cy, cz = sizes
        pitch = cy + 4
        x_rows = up(3 * cx * cy + 2) + up(cx * cy)
        y_rows = up(6 * cx + 2) + up(2 * cx)
        rows = up(2 * (pitch + 1) + up((cx + 2) * pitch + cy + 3 - (pitch + 1)))
        f32 = jnp.float32
        vmem = pl.BlockSpec(memory_space=pltpu.VMEM)
        return pl.pallas_call(
            functools.partial(kernel, sizes, counts),
            out_shape=(jax.ShapeDtypeStruct((3,) + sizes, f32), jax.ShapeDtypeStruct(sizes, f32)),
            in_specs=[vmem] * 3,
            out_specs=(vmem, vmem),
            scratch_shapes=[
                pltpu.VMEM((ITERS, x_rows, LANES), f32),
                pltpu.VMEM((ITERS, 2, y_rows, LANES), f32),
                pltpu.VMEM((ITERS, 2, 2, LANES), f32),
                pltpu.VMEM((ITERS, 2, x_rows, LANES), f32),
                pltpu.VMEM((ITERS, 3, 2, y_rows, LANES), f32),
                pltpu.VMEM((ITERS, 9, 2, 2, LANES), f32),
                pltpu.VMEM((LANES, LANES), f32),
                pltpu.VMEM((3, 4, rows, LANES), f32),
                pltpu.VMEM((9, 8, LANES), f32),
                pltpu.VMEM((4, rows, LANES), f32),
                pltpu.SemaphoreType.DMA((ITERS, len(NEAR))),
                pltpu.SemaphoreType.DMA((ITERS, len(NEAR))),
            ],
            compiler_params=pltpu.CompilerParams(collective_id=0, has_side_effects=True),
        )(displace, occupied, strength)

    in_specs = (P(None, "gx", "gy", "gz"), P("gx", "gy", "gz"), P("gx", "gy", "gz"))
    out_specs = (P(None, "gx", "gy", "gz"), P("gx", "gy", "gz"))
    return jax.shard_map(body, mesh=mesh, in_specs=in_specs, out_specs=out_specs, check_vma=False)
```

time: 98 us -> 23.9 us (0.24)
  the two profiles are of different devices: /device:TPU:14 before, /device:TPU:1 now
where the time goes in v1:
time: 23.9 us; the launch traced here: 23.7 us
  Pallas kernels  21.1 us (88%)
  local copies, waits for them, and re-layouts  1.95 us (8%)
  between operations  0.65 us (3%)
    pallas_call x1, Pallas kernels, body(): pl.pallas_call(functools.partial(kernel, sizes, counts), out_shape=(jax.S...  21.1 us
    unnamed x4, local copies, waits for them, and re-layouts  1.95 us

profile of v1, /device:TPU:1, one launch (start us, length us, event | category | flops | bytes accessed | tf_op | source)
XLA Modules:
  0.0 23.7 jit_solution(5226991179029221108)
XLA Ops:
  0.6 21.1 %shard_map.50 = (f32[3,2,8,128]{3,2,1,0:T(8,128)}, f32[2,8,128]{2,1,0:T(8,128)}) custom-call(f32[3,2,8,128]{3,2,1,0:T(8,128)} %disp_ref.1, s32[2,8,128]{2,1,0:T(8,128)} %occ_ref.1, f32[2,8,128]{2,1,0:T(8,128)} %str_ref.1), custom_call_target="tpu_custom_call" | custom-call | tf_op jit(solution)/shard_map/pallas_call | solution.py:315
  21.7 0.0 copy-start
  21.7 1.4 %copy.7 = f32[3,2,8,128]{3,2,1,0:T(8,128)} copy(f32[3,2,8,128]{3,2,1,0:T(8,128)} %get-tuple-element.4) | data formatting | bytes 49152
  23.1 0.0 copy-done
  23.1 0.6 %copy.8 = f32[2,8,128]{2,1,0:T(8,128)} copy(f32[2,8,128]{2,1,0:T(8,128)S(1)} %copy-done) | data formatting | bytes 16384
Async XLA Ops:
  21.7 1.4 %copy-start = (f32[2,8,128]{2,1,0:T(8,128)S(1)}, f32[2,8,128]{2,1,0:T(8,128)}, u32[]{:S(2)}) copy-start(f32[2,8,128]{2,1,0:T(8,128)} %get-tuple-element.5) | copy-start | bytes 24580

commit v2 on v1

--- a/solution.py
+++ b/solution.py
@@ -29,8 +29,9 @@
     return -(-rows // 8) * 8
 
 
-def kernel(sizes, counts, disp_ref, occ_ref, str_ref, force_ref, energy_ref,
-           xs, ys, zs, xl, yl, zl, stage, near, cols, slopes, send_sem, recv_sem):
+def kernel(sizes, counts, disp_hbm, occ_hbm, str_hbm, force_ref, energy_ref,
+           xs, ys, zs, xl, yl, zl, stage, near, cols, slopes, disp_ref, occ_ref, str_ref,
+           send_sem, recv_sem, load_sem):
     cx, cy, cz = sizes
     pitch = cy + 4
     group = LANES // 4
@@ -39,6 +40,12 @@
     xw, yw = up(xu + 2), up(yu + 2)
     x_rows = (xs.shape[1], xw)
     y_rows = (ys.shape[2], yw)
+
+    loads = [pltpu.make_async_copy(disp_hbm, disp_ref, load_sem.at[0]),
+             pltpu.make_async_copy(occ_hbm, occ_ref, load_sem.at[1]),
+             pltpu.make_async_copy(str_hbm, str_ref, load_sem.at[2])]
+    for load in loads:
+        load.start()
 
     me = [lax.axis_index(axis) for axis in AXES]
     there = [[None if s == 0 else (m + s >= 0) & (m + s < n) for s in (-1, 0, 1)]
@@ -75,8 +82,8 @@
             src = xs.at[t, pl.ds(0, rows)]
             dst = xl.at[t, 0 if o[0] == 1 else 1, pl.ds(0, rows)]
         return pltpu.make_async_remote_copy(
-            src_ref=src, dst_ref=dst, send_sem=send_sem.at[t, SLOT[o]],
-            recv_sem=recv_sem.at[t, SLOT[back]], device_id=target(o), device_id_type=MESH)
+            src_ref=src, dst_ref=dst, send_sem=send_sem.at[SLOT[o]],
+            recv_sem=recv_sem.at[t % 2, SLOT[back]], device_id=target(o), device_id_type=MESH)
 
     for o in NEAR:
         @pl.when(jnp.logical_not(exists(o)))
@@ -93,6 +100,8 @@
     near[...] = jnp.zeros(near.shape, jnp.float32)
     cols[...] = jnp.zeros(cols.shape, jnp.float32)
 
+    for load in loads:
+        load.wait()
     mine = [[disp_ref[q, x] for x in range(cx)] for q in range(3)]
     mine.append([occ_ref[x].astype(jnp.float32) * str_ref[x] for x in range(cx)])
 
@@ -147,6 +156,7 @@
             @pl.when(exists(o))
             def _(o=o):
                 ends(t, minus(o)).wait_recv()
+                ends(t, o).wait_send()
 
         quantities = range(4) if t == 0 else range(3)
         for q in quantities:
@@ -293,12 +303,6 @@
                 for q in range(3):
                     mine[q][x] = here[q] + STEP * force[q]
 
-    for t in range(ITERS):
-        for o in NEAR:
-            @pl.when(exists(o))
-            def _(o=o, t=t):
-                ends(t, o).wait_send()
-
 
 def solution(mesh):
     counts = tuple(mesh.shape[axis] for axis in AXES)
@@ -314,8 +318,8 @@
         vmem = pl.BlockSpec(memory_space=pltpu.VMEM)
         return pl.pallas_call(
             functools.partial(kernel, sizes, counts),
-            out_shape=(jax.ShapeDtypeStruct((3,) + sizes, f32), jax.ShapeDtypeStruct(sizes, f32)),
-            in_specs=[vmem] * 3,
+            out_shape=(pltpu.VMEM((3,) + sizes, f32), pltpu.VMEM(sizes, f32)),
+            in_specs=[pl.BlockSpec(memory_space=pl.ANY)] * 3,
             out_specs=(vmem, vmem),
             scratch_shapes=[
                 pltpu.VMEM((ITERS, x_rows, LANES), f32),
@@ -328,8 +332,12 @@
                 pltpu.VMEM((3, 4, rows, LANES), f32),
                 pltpu.VMEM((9, 8, LANES), f32),
                 pltpu.VMEM((4, rows, LANES), f32),
-                pltpu.SemaphoreType.DMA((ITERS, len(NEAR))),
-                pltpu.SemaphoreType.DMA((ITERS, len(NEAR))),
+                pltpu.VMEM((3,) + sizes, f32),
+                pltpu.VMEM(sizes, jnp.int32),
+                pltpu.VMEM(sizes, f32),
+                pltpu.SemaphoreType.DMA((len(NEAR),)),
+                pltpu.SemaphoreType.DMA((2, len(NEAR))),
+                pltpu.SemaphoreType.DMA((3,)),
             ],
             compiler_params=pltpu.CompilerParams(collective_id=0, has_side_effects=True),
         )(displace, occupied, strength)

time: 23.9 us -> 21.1 us (0.88)
  Pallas kernels: 21.1 us -> 19.1 us
  local copies, waits for them, and re-layouts: 1.95 us -> 1.21 us
    pallas_call x1, Pallas kernels: 21.1 us -> 19.1 us  [body(): pl.pallas_call(functools.partial(kernel, sizes, counts), out_shape=(pltpu...]
    unnamed x4 -> x2, local copies, waits for them, and re-layouts: 1.95 us -> 1.21 us
where the time goes in v2:
time: 21.1 us; the launch traced here: 20.9 us
  Pallas kernels  19.1 us (91%)
  local copies, waits for them, and re-layouts  1.21 us (6%)
  between operations  0.64 us (3%)
    pallas_call x1, Pallas kernels, body(): pl.pallas_call(functools.partial(kernel, sizes, counts), out_shape=(pltpu...  19.1 us
    unnamed x2, local copies, waits for them, and re-layouts  1.21 us

profile of v2, /device:TPU:1, one launch (start us, length us, event | category | flops | bytes accessed | tf_op | source)
XLA Modules:
  0.0 20.9 jit_solution(7458522799961060727)
XLA Ops:
  0.6 19.1 %shard_map.50 = (f32[3,2,8,128]{3,2,1,0:T(8,128)S(1)}, f32[2,8,128]{2,1,0:T(8,128)S(1)}) custom-call(f32[3,2,8,128]{3,2,1,0:T(8,128)} %disp_hbm.1, s32[2,8,128]{2,1,0:T(8,128)} %occ_hbm.1, f32[2,8,128]{2,1,0:T(8,128)} %str_hbm.1), custom_call_target="tpu_custom_call" | custom-call | tf_op jit(solution)/shard_map/pallas_call | solution.py:319
  19.7 0.6 %copy.7 = f32[3,2,8,128]{3,2,1,0:T(8,128)} copy(f32[3,2,8,128]{3,2,1,0:T(8,128)S(1)} %get-tuple-element.2) | data formatting | bytes 49152
  20.3 0.6 %copy.8 = f32[2,8,128]{2,1,0:T(8,128)} copy(f32[2,8,128]{2,1,0:T(8,128)S(1)} %get-tuple-element.3) | data formatting | bytes 16384

commit v3 on v2

--- a/solution.py
+++ b/solution.py
@@ -18,7 +18,6 @@
     ((dx, dy, dz) for dx, dy in PLANE for dz in (-1, 0, 1) if (dx, dy, dz) != (0, 0, 0)),
     key=lambda o: (-sum(abs(a) for a in o), o),
 )
-SLOT = {o: i for i, o in enumerate(NEAR)}
 
 
 def minus(o):
@@ -31,7 +30,7 @@
 
 def kernel(sizes, counts, disp_hbm, occ_hbm, str_hbm, force_ref, energy_ref,
            xs, ys, zs, xl, yl, zl, stage, near, cols, slopes, disp_ref, occ_ref, str_ref,
-           send_sem, recv_sem, load_sem):
+           zero, zero_row, sink_x, sink_y, sink_z, tally, send_sem, recv_sem, load_sem):
     cx, cy, cz = sizes
     pitch = cy + 4
     group = LANES // 4
@@ -82,20 +81,27 @@
             src = xs.at[t, pl.ds(0, rows)]
             dst = xl.at[t, 0 if o[0] == 1 else 1, pl.ds(0, rows)]
         return pltpu.make_async_remote_copy(
-            src_ref=src, dst_ref=dst, send_sem=send_sem.at[SLOT[o]],
-            recv_sem=recv_sem.at[t % 2, SLOT[back]], device_id=target(o), device_id_type=MESH)
-
-    for o in NEAR:
-        @pl.when(jnp.logical_not(exists(o)))
-        def _(o=o):
-            if o[2] != 0:
-                spot = zl.at[:, PLANE.index(o[:2]), 0 if o[2] == -1 else 1]
-            elif o[1] != 0:
-                spot = yl.at[:, o[0] + 1, 0 if o[1] == -1 else 1]
-            else:
-                spot = xl.at[:, 0 if o[0] == -1 else 1]
-            spot[...] = jnp.zeros(spot.shape, jnp.float32)
-
+            src_ref=src, dst_ref=dst, send_sem=send_sem,
+            recv_sem=recv_sem.at[t % 2], device_id=target(o), device_id_type=MESH)
+
+    def fill(t, o):
+        if o[2] != 0:
+            j, side = PLANE.index(o[:2]), 0 if o[2] == -1 else 1
+            src, spot, sink = zero_row, zl.at[t, j, side], sink_z.at[j, side]
+        elif o[1] != 0:
+            rows = pl.ds(0, y_rows[0] if t == 0 else y_rows[1])
+            side = 0 if o[1] == -1 else 1
+            src, spot = zero.at[rows], yl.at[t, o[0] + 1, side, rows]
+            sink = sink_y.at[o[0] + 1, side, rows]
+        else:
+            rows = pl.ds(0, x_rows[0] if t == 0 else x_rows[1])
+            side = 0 if o[0] == -1 else 1
+            src, spot, sink = zero.at[rows], xl.at[t, side, rows], sink_x.at[side, rows]
+        pltpu.make_async_copy(src, spot, recv_sem.at[t % 2]).start()
+        pltpu.make_async_copy(src, sink, send_sem).start()
+
+    zero[...] = jnp.zeros(zero.shape, jnp.float32)
+    zero_row[...] = jnp.zeros(zero_row.shape, jnp.float32)
     stage[...] = jnp.zeros(stage.shape, jnp.float32)
     near[...] = jnp.zeros(near.shape, jnp.float32)
     cols[...] = jnp.zeros(cols.shape, jnp.float32)
@@ -152,11 +158,14 @@
             @pl.when(exists(o))
             def _(o=o):
                 ends(t, o).start()
-        for o in reversed(NEAR):
-            @pl.when(exists(o))
+
+            @pl.when(jnp.logical_not(exists(o)))
             def _(o=o):
-                ends(t, minus(o)).wait_recv()
-                ends(t, o).wait_send()
+                fill(t, o)
+        pick = 0 if t == 0 else 1
+        bytes_of = tally.at[pl.ds(0, (2 * x_rows[pick] + 6 * y_rows[pick] + 36) // 4)]
+        pltpu.make_async_copy(bytes_of, bytes_of, recv_sem.at[t % 2]).wait()
+        pltpu.make_async_copy(bytes_of, bytes_of, send_sem).wait()
 
         quantities = range(4) if t == 0 else range(3)
         for q in quantities:
@@ -335,8 +344,14 @@
                 pltpu.VMEM((3,) + sizes, f32),
                 pltpu.VMEM(sizes, jnp.int32),
                 pltpu.VMEM(sizes, f32),
-                pltpu.SemaphoreType.DMA((len(NEAR),)),
-                pltpu.SemaphoreType.DMA((2, len(NEAR))),
+                pltpu.VMEM((x_rows, LANES), f32),
+                pltpu.VMEM((2, LANES), f32),
+                pltpu.VMEM((2, x_rows, LANES), f32),
+                pltpu.VMEM((3, 2, y_rows, LANES), f32),
+                pltpu.VMEM((9, 2, 2, LANES), f32),
+                pltpu.VMEM(((2 * x_rows + 6 * y_rows + 36) // 4, 4, LANES), f32),
+                pltpu.SemaphoreType.DMA,
+                pltpu.SemaphoreType.DMA((2,)),
                 pltpu.SemaphoreType.DMA((3,)),
             ],
             compiler_params=pltpu.CompilerParams(collective_id=0, has_side_effects=True),

time: 21.1 us -> 20.6 us (0.976)
  Pallas kernels: 19.1 us -> 18.6 us
    pallas_call x1, Pallas kernels: 19.1 us -> 18.6 us  [body(): pl.pallas_call(functools.partial(kernel, sizes, counts), out_shape=(pltpu...]
where the time goes in v3:
time: 20.6 us; the launch traced here: 20.5 us
  Pallas kernels  18.6 us (90%)
  local copies, waits for them, and re-layouts  1.21 us (6%)
  between operations  0.64 us (3%)
    pallas_call x1, Pallas kernels, body(): pl.pallas_call(functools.partial(kernel, sizes, counts), out_shape=(pltpu...  18.6 us
    unnamed x2, local copies, waits for them, and re-layouts  1.21 us

profile of v3, /device:TPU:1, one launch (start us, length us, event | category | flops | bytes accessed | tf_op | source)
XLA Modules:
  0.0 20.5 jit_solution(15691228501227334670)
XLA Ops:
  0.6 18.6 %shard_map.50 = (f32[3,2,8,128]{3,2,1,0:T(8,128)S(1)}, f32[2,8,128]{2,1,0:T(8,128)S(1)}) custom-call(f32[3,2,8,128]{3,2,1,0:T(8,128)} %disp_hbm.1, s32[2,8,128]{2,1,0:T(8,128)} %occ_hbm.1, f32[2,8,128]{2,1,0:T(8,128)} %str_hbm.1), custom_call_target="tpu_custom_call" | custom-call | tf_op jit(solution)/shard_map/pallas_call | solution.py:328
  19.3 0.6 %copy.7 = f32[3,2,8,128]{3,2,1,0:T(8,128)} copy(f32[3,2,8,128]{3,2,1,0:T(8,128)S(1)} %get-tuple-element.2) | data formatting | bytes 49152
  19.9 0.6 %copy.8 = f32[2,8,128]{2,1,0:T(8,128)} copy(f32[2,8,128]{2,1,0:T(8,128)S(1)} %get-tuple-element.3) | data formatting | bytes 16384
